TPU v7x, 256 devices: a whole 4x4x8 slice. The times are simulated.
256 devices in a mesh: ex: 8 (over z), ctx: 32 (over x, y, core).
Axes of the slice: x: 4, y: 4, z: 8, core: 2. Of those that a mesh axis runs over, the one named last changes fastest.
Arguments:
- stream: bfloat16 [8, 256, 32768], P('ex', None, 'ctx'), may hold values from -6 to 6
- cotangent: bfloat16 [8, 256, 32768], P('ex', None, 'ctx'), may hold values from -6 to 6
- base_ids: int32 [8, 32768], P('ex', 'ctx'), may hold values from 0 to 4
- clip_bound: int32 [8], P('ex'), may hold values from 1 to 4
- w_value: bfloat16 [256, 256], replicated, may hold values from -2 to 2
- w_gate: bfloat16 [256, 256], replicated, may hold values from -0.375 to 0.375
- filter_taps: float32 [256, 32768], P('ctx', 'ex'), may hold values from -0.03125 to 0.03125
- filter_bias: float32 [256], P('ctx'), may hold values from 0.1 to 1.9
Outputs:
- input_grad: bfloat16 [8, 256, 32768], P('ex', None, 'ctx')
- filter_grad: float32 [256, 32768], P('ctx', 'ex')
All inputs are finite; a program needn't handle non-finite values.
Results may differ from a plain program's by a relative error of at most 0.015.
Values may be sent and summed in bfloat16 or wider, within the bound.
No kernel may reach another device: no remote copies, remote signals or barrier semaphores. Data moves between devices by JAX's collectives and lax.ppermute only.
A program may use at most 128 MiB of HBM per device.

v0:
```python
import math
import jax
import jax.numpy as jnp
from jax import lax
from jax.sharding import PartitionSpec as P

RADIX = 128
unknown_base = 4
norm_eps = 1e-06


def joined_along(parts, dim):
    lengths = list(parts.shape[1:])
    lengths[dim] *= parts.shape[0]
    return jnp.moveaxis(parts, 0, dim).reshape(lengths)


def from_everyone(x, axis):
    copies = jnp.broadcast_to(x, (lax.axis_size(axis), *x.shape))
    return lax.all_to_all(copies, axis, split_axis=0, concat_axis=0, tiled=True)


def gathered_copies(x, axis, dim):
    return joined_along(from_everyone(x, axis), dim)


def over_copies(x, axis):
    return from_everyone(x, axis).sum(axis=0)


def cut_along(x, dim, size):
    before, after = (x.shape[:dim], x.shape[dim + 1 :])
    return jnp.moveaxis(x.reshape(*before, size, -1, *after), dim, 0)


def sum_at_owner(x, axis, dim):
    size = lax.axis_size(axis)
    parts = lax.all_to_all(cut_along(x, dim, size), axis, 0, 0, tiled=True)
    return jnp.sum(parts.astype(jnp.float32), axis=0)


def dft_table(order):
    indices = jnp.arange(order, dtype=jnp.int32)
    phase_angle = (indices[:, None] * indices[None, :] % order).astype(jnp.float32) * (
        2.0 * math.pi / order
    )
    return (jnp.cos(phase_angle), jnp.sin(phase_angle))


def twiddle_table(outer, inner):
    whole = outer * inner
    outer_idx = jnp.arange(outer, dtype=jnp.int32)
    inner_idx = jnp.arange(inner, dtype=jnp.int32)
    phase_angle = (outer_idx[:, None] * inner_idx[None, :] % whole).astype(jnp.float32) * (
        2.0 * math.pi / whole
    )
    return (jnp.cos(phase_angle), jnp.sin(phase_angle))


def first_section(signal, cos_long, sin_long, first_block, radix_size):
    channels = signal.shape[0]
    number_blocks = signal.shape[1] // radix_size
    shaped = signal.reshape(channels, number_blocks, radix_size)
    cos_rows = lax.dynamic_slice_in_dim(cos_long, first_block, number_blocks, 0)
    sin_rows = lax.dynamic_slice_in_dim(sin_long, first_block, number_blocks, 0)
    real_part = jnp.einsum("cbk,bf->ckf", shaped, cos_rows)
    imag_part = -jnp.einsum("cbk,bf->ckf", shaped, sin_rows)
    return (real_part, imag_part)


def second_section(real_part, imag_part, tables):
    cos_long, sin_long, cos_short, sin_short, cos_twist, sin_twist = tables
    twist_real = real_part * cos_twist + imag_part * sin_twist
    twist_imag = imag_part * cos_twist - real_part * sin_twist
    out_real = jnp.einsum("fk,ckg->cfg", cos_short, twist_real)
    out_real = out_real + jnp.einsum("fk,ckg->cfg", sin_short, twist_imag)
    out_imag = jnp.einsum("fk,ckg->cfg", cos_short, twist_imag)
    out_imag = out_imag - jnp.einsum("fk,ckg->cfg", sin_short, twist_real)
    return (out_real, out_imag)


def forward_full(signal, tables, radix_size):
    real_part, imag_part = first_section(signal, tables[0], tables[1], 0, radix_size)
    return second_section(real_part, imag_part, tables)


def inverse_half(real_part, imag_part, tables, half_blocks):
    cos_long, sin_long, cos_short, sin_short, cos_twist, sin_twist = tables
    mid_real = jnp.einsum("tf,cfg->ctg", cos_short, real_part)
    mid_real = mid_real - jnp.einsum("tf,cfg->ctg", sin_short, imag_part)
    mid_imag = jnp.einsum("tf,cfg->ctg", cos_short, imag_part)
    mid_imag = mid_imag + jnp.einsum("tf,cfg->ctg", sin_short, real_part)
    twist_real = mid_real * cos_twist - mid_imag * sin_twist
    twist_imag = mid_real * sin_twist + mid_imag * cos_twist
    cos_cols = cos_long[:, :half_blocks]
    sin_cols = sin_long[:, :half_blocks]
    outputs = jnp.einsum("ckg,gt->ctk", twist_real, cos_cols)
    outputs = outputs - jnp.einsum("ckg,gt->ctk", twist_imag, sin_cols)
    whole = cos_short.shape[0] * cos_long.shape[0]
    return outputs.reshape(outputs.shape[0], -1) * (1.0 / whole)


def on_device(stream, cotangent, base_ids, clip_bound, w_value, w_gate, filter_taps, filter_bias):
    tokens_in = stream[0]
    value_tok = jnp.dot(w_value, tokens_in, preferred_element_type=jnp.float32).astype(jnp.bfloat16)
    gate_tok = jnp.dot(w_gate, tokens_in, preferred_element_type=jnp.float32).astype(jnp.bfloat16)
    keep_mask = (base_ids[0] != unknown_base).astype(jnp.float32)
    cot_tok = cotangent[0].astype(jnp.float32) * keep_mask[None, :]
    signal_tok = (gate_tok.astype(jnp.float32) * cot_tok).astype(jnp.bfloat16)
    radix_size = RADIX
    seq_len = tokens_in.shape[1] * lax.axis_size("ctx")
    long_order = 2 * seq_len // radix_size
    half_blocks = long_order // 2
    cos_long, sin_long = dft_table(long_order)
    cos_short, sin_short = dft_table(radix_size)
    cos_twist, sin_twist = twiddle_table(radix_size, long_order)
    tables = (cos_long, sin_long, cos_short, sin_short, cos_twist, sin_twist)
    channels = filter_taps.shape[0]
    zeros_spec = jnp.zeros((channels, radix_size, long_order), jnp.float32)
    first_block = jnp.int32(0) // radix_size
    real_part, imag_part = first_section(
        gathered_copies(filter_taps.astype(jnp.bfloat16), "ex", 1).astype(filter_taps.dtype),
        cos_long,
        sin_long,
        first_block,
        radix_size,
    )
    taps_real = zeros_spec + real_part
    taps_imag = zeros_spec + imag_part
    filt_real, filt_imag = second_section(taps_real, taps_imag, tables)
    value_ch, signal_ch = (
        lax.all_to_all(value_tok, "ctx", split_axis=0, concat_axis=1, tiled=True),
        lax.all_to_all(signal_tok, "ctx", split_axis=0, concat_axis=1, tiled=True),
    )
    value_wide = value_ch.astype(jnp.float32)
    signal_wide = signal_ch.astype(jnp.float32)
    val_real, val_imag = forward_full(value_wide, tables, radix_size)
    grad_real, grad_imag = forward_full(signal_wide, tables, radix_size)
    bias_col = filter_bias[:, None]
    conv_out = inverse_half(
        filt_real * val_real - filt_imag * val_imag,
        filt_real * val_imag + filt_imag * val_real,
        tables,
        half_blocks,
    )
    conv_state = (conv_out + bias_col * value_wide).astype(jnp.bfloat16)
    back_out = inverse_half(
        filt_real * grad_real + filt_imag * grad_imag,
        filt_real * grad_imag - filt_imag * grad_real,
        tables,
        half_blocks,
    )
    value_grad_ch = (back_out + bias_col * signal_wide).astype(jnp.bfloat16)
    taps_grad = inverse_half(
        grad_real * val_real + grad_imag * val_imag,
        grad_imag * val_real - grad_real * val_imag,
        tables,
        half_blocks,
    )
    value_grad_tok, state_tok = (
        lax.all_to_all(value_grad_ch, "ctx", split_axis=1, concat_axis=0, tiled=True),
        lax.all_to_all(conv_state, "ctx", split_axis=1, concat_axis=0, tiled=True),
    )
    gate_grad_tok = (state_tok.astype(jnp.float32) * cot_tok).astype(jnp.bfloat16)
    input_grad = jnp.dot(w_value.T, value_grad_tok, preferred_element_type=jnp.float32)
    input_grad = input_grad + jnp.dot(w_gate.T, gate_grad_tok, preferred_element_type=jnp.float32)
    input_grad = input_grad.astype(jnp.bfloat16)[None]
    width = w_value.shape[0]
    entries = float(seq_len * width)
    square_sum = jnp.sum(taps_grad * taps_grad)
    bound_value = clip_bound[0].astype(jnp.float32)
    grand_total = over_copies(square_sum, "ctx")
    factor = jnp.minimum(1.0, bound_value / jnp.sqrt(grand_total / entries + norm_eps))
    filter_grad = sum_at_owner((factor * taps_grad).astype(jnp.bfloat16), "ex", 1)
    return (input_grad, filter_grad)


def solution(mesh):
    in_specs = (
        P("ex", None, "ctx"),
        P("ex", None, "ctx"),
        P("ex", "ctx"),
        P("ex"),
        P(),
        P(),
        P("ctx", "ex"),
        P("ctx"),
    )
    out_specs = (P("ex", None, "ctx"), P("ctx", "ex"))
    return jax.shard_map(
        on_device, mesh=mesh, in_specs=in_specs, out_specs=out_specs, check_vma=False
    )
```

profile of v0, /device:TPU:1, one launch (start us, length us, event | category | flops | bytes accessed | tf_op | source)
XLA Modules:
  0.0 182.3 jit_solution(5698253643525853579)
XLA Ops:
  0.7 0.8 compare_convert_fusion
  1.7 2.3 %fusion.88 = bf16[32,8,1024]{2,1,0:T(8,128)(2,1)} fusion(bf16[256,256]{1,0:T(8,128)(2,1)} %param.13, bf16[1,256,1024]{2,1,0:T(8,128)(2,1)} %param.9, bf16[1,256,1024]{2,1,0:T(8,128)(2,1)S(1)} %copy-done, f32[1024]{0:T(1024)S(1)} %bitcast.287), kind=kOutput, calls=%fused_computation.94 | convolution fusion | flops 135790592 | bytes 1708032 | tf_op jit(solution)/shard_map/dot_general | solution.py:106
  4.0 8.6 %all-to-all-start.1 = ((bf16[32,8,1024]{2,1,0:T(8,128)(2,1)}), bf16[32,8,1024]{2,1,0:T(8,128)(2,1)S(1)}, u32[]{:S(2)}, u32[]{:S(2)}) async-start(bf16[32,8,1024]{2,1,0:T(8,128)(2,1)} %fusion.88), calls=%async_computation.1 | async-start | bytes 1048576 | tf_op jit(solution)/shard_map/all_to_all | solution.py:133
  12.6 1.0 fusion.143
  13.6 4.6 %fusion.120 = bf16[512,512]{0,1:T(8,128)(2,1)} fusion(), kind=kLoop, calls=%fused_computation.137 | loop fusion | flops 3932160 | bytes 524288 | tf_op jit(solution)/shard_map/cos | solution.py:47
  18.2 4.6 %fusion.119 = bf16[512,512]{0,1:T(8,128)(2,1)} fusion(), kind=kLoop, calls=%fused_computation.136 | loop fusion | flops 3932160 | bytes 524288 | tf_op jit(solution)/shard_map/sin | solution.py:47
  22.8 1.1 fusion.89
  24.1 7.2 %all-to-all-start.3 = ((bf16[32,8,1024]{2,1,0:T(8,128)(2,1)}), bf16[32,8,1024]{2,1,0:T(8,128)(2,1)}, u32[]{:S(2)}, u32[]{:S(2)}) async-start(bf16[32,8,1024]{2,1,0:T(8,128)(2,1)} %fusion.89), calls=%async_computation.3 | async-start | bytes 1048576 | tf_op jit(solution)/shard_map/all_to_all | solution.py:132
  31.7 1.0 reshape.97
  32.7 1.6 fusion.122
  34.3 1.8 fusion.125
  36.1 6.9 %all-to-all-done.3 = bf16[32,8,1024]{2,1,0:T(8,128)(2,1)} async-done(((bf16[32,8,1024]{2,1,0:T(8,128)(2,1)}), bf16[32,8,1024]{2,1,0:T(8,128)(2,1)}, u32[]{:S(2)}, u32[]{:S(2)}) %all-to-all-start.3) | async-done | bytes 524320 | tf_op jit(solution)/shard_map/all_to_all | solution.py:132
  43.0 0.8 broadcast_in_dim.6
  43.8 8.2 %all-to-all-start = ((bf16[8,8,4096]{2,1,0:T(8,128)(2,1)}), bf16[8,8,4096]{2,1,0:T(8,128)(2,1)}, u32[]{:S(2)}, u32[]{:S(2)}) async-start(bf16[8,8,4096]{2,1,0:T(8,128)(2,1)} %broadcast_in_dim.6), calls=%async_computation | async-start | bytes 1048576 | tf_op jit(solution)/shard_map/all_to_all | solution.py:20
  52.0 2.1 %copy.144 = bf16[8,32,1024]{2,1,0:T(8,128)(2,1)} copy(bf16[8,32,1024]{2,0,1:T(8,128)(2,1)} %bitcast.24) | data formatting | bytes 1048576 | tf_op jit(solution)/shard_map/all_to_all | solution.py:132
  54.1 2.1 %reshape.98 = bf16[8,256,128]{2,1,0:T(8,128)(2,1)} reshape(bf16[8,32,1024]{2,1,0:T(8,128)(2,1)} %copy.144) | data formatting | bytes 1048576 | tf_op jit(solution)/shard_map/reshape | solution.py:63
  56.2 1.6 fusion.121
  58.2 0.8 fusion.129
  59.0 0.8 fusion.130
  59.9 0.8 copy-done.2
  60.6 0.8 fusion.127
  61.4 2.2 %convolution_add_fusion.1 = f32[8,512,128]{2,1,0:T(8,128)} fusion(f32[8,512,128]{2,1,0:T(8,128)S(1)} %fusion.127, f32[8,128,512]{1,2,0:T(8,128)S(1)} %fusion.122, f32[8,128,512]{1,2,0:T(8,128)S(1)} %copy-done.2, f32[128,512]{0,1:T(8,128)S(1)} %get-tuple-element.28, f32[128,512]{0,1:T(8,128)S(1)} %get-tuple-element.29), kind=kOutput, calls=%fused_computation.74 | convolution fusion | flops 137068544 | bytes 8912896 | tf_op jit(solution)/shard_map/fk,ckg->cfg/dot_general | solution.py:76
  63.6 2.1 %fusion.128 = f32[8,512,128]{2,1,0:T(8,128)} fusion(f32[8,128,512]{1,2,0:T(8,128)S(1)} %fusion.122, f32[8,128,512]{1,2,0:T(8,128)S(1)} %copy-done.2, f32[128,512]{0,1:T(8,128)S(1)} %get-tuple-element.28, f32[128,512]{0,1:T(8,128)S(1)} %get-tuple-element.29), kind=kOutput, calls=%fused_computation.148 | convolution fusion | flops 136544256 | bytes 6815744 | tf_op jit(solution)/shard_map/fk,ckg->cfg/dot_general | solution.py:77
  65.8 2.3 %convolution_add_fusion = f32[8,512,128]{2,1,0:T(8,128)} fusion(f32[8,512,128]{2,1,0:T(8,128)S(1)} %fusion.129, f32[8,128,512]{1,2,0:T(8,128)S(1)} %fusion.121, f32[8,128,512]{1,2,0:T(8,128)S(1)} %fusion.124, f32[128,512]{0,1:T(8,128)S(1)} %get-tuple-element.28, f32[128,512]{0,1:T(8,128)S(1)} %get-tuple-element.29), kind=kOutput, calls=%fused_computation.71 | convolution fusion | flops 137068544 | bytes 8912896 | tf_op jit(solution)/shard_map/fk,ckg->cfg/dot_general | solution.py:76
  68.0 2.2 %convolution_subtract_fusion = f32[8,512,128]{2,1,0:T(8,128)} fusion(f32[8,512,128]{2,1,0:T(8,128)S(1)} %fusion.130, f32[8,128,512]{1,2,0:T(8,128)S(1)} %fusion.121, f32[8,128,512]{1,2,0:T(8,128)S(1)} %fusion.124, f32[128,512]{0,1:T(8,128)S(1)} %get-tuple-element.28, f32[128,512]{0,1:T(8,128)S(1)} %get-tuple-element.29), kind=kOutput, calls=%fused_computation.70 | convolution fusion | flops 137068544 | bytes 8912896 | tf_op jit(solution)/shard_map/fk,ckg->cfg/dot_general | solution.py:78
  70.3 2.1 %copy.132 = bf16[8,8,4096]{2,1,0:T(8,128)(2,1)} copy(bf16[8,8,4096]{2,0,1:T(8,128)(2,1)} %bitcast.2) | data formatting | bytes 1048576 | tf_op jit(solution)/shard_map/transpose | solution.py:15
  72.4 2.1 %reshape.96 = bf16[8,256,128]{2,1,0:T(8,128)(2,1)} reshape(bf16[8,8,4096]{2,1,0:T(8,128)(2,1)} %copy.132) | data formatting | bytes 1048576 | tf_op jit(solution)/shard_map/reshape | solution.py:63
  74.5 1.6 fusion.123
  76.6 0.8 fusion.135
  77.4 0.8 fusion.131
  78.2 0.9 convolution_add_fusion.2
  79.1 0.9 convolution_subtract_fusion.2
  80.0 0.8 copy-done.3
  80.8 0.6 copy-done.7
  81.4 0.6 copy-done.8
  82.6 3.8 %multiply_add_fusion = (bf16[8,512,128]{2,1,0:T(8,128)(2,1)S(1)}, bf16[8,512,128]{2,1,0:T(8,128)(2,1)S(1)}, bf16[8,512,128]{2,1,0:T(8,128)(2,1)S(1)}, bf16[8,512...) fusion(f32[8,512,128]{2,1,0:T(8,128)S(1)} %copy-done.9, ...), kind=kOutput, calls=%fused_computation.55 | convolution fusion | flops 149651456 | bytes 23592960 | tf_op jit(solution)/shard_map/fk,ckg->cfg/dot_general | solution.py:78
  86.4 0.7 fusion.8
  87.1 0.7 fusion.6
  87.7 2.1 %fusion.36 = f32[8,512,128]{2,1,0:T(8,128)} fusion(bf16[8,512,128]{2,1,0:T(8,128)(2,1)S(1)} %get-tuple-element.22), kind=kOutput, calls=%fused_computation.42 | convolution fusion | flops 134447104 | bytes 3145728 | tf_op jit(solution)/shard_map/tf,cfg->ctg/dot_general | solution.py:90
  89.8 2.0 %fusion.34 = f32[8,512,128]{2,1,0:T(8,128)} fusion(bf16[8,512,128]{2,1,0:T(8,128)(2,1)S(1)} %get-tuple-element.22), kind=kOutput, calls=%fused_computation.40 | convolution fusion | flops 134447104 | bytes 3145728 | tf_op jit(solution)/shard_map/tf,cfg->ctg/dot_general | solution.py:91
  91.8 2.0 %fusion.22 = f32[8,512,128]{2,1,0:T(8,128)} fusion(bf16[8,512,128]{2,1,0:T(8,128)(2,1)S(1)} %get-tuple-element.20), kind=kOutput, calls=%fused_computation.26 | convolution fusion | flops 134447104 | bytes 3145728 | tf_op jit(solution)/shard_map/tf,cfg->ctg/dot_general | solution.py:90
  93.8 2.0 %fusion.20 = f32[8,512,128]{2,1,0:T(8,128)} fusion(bf16[8,512,128]{2,1,0:T(8,128)(2,1)S(1)} %get-tuple-element.20), kind=kOutput, calls=%fused_computation.24 | convolution fusion | flops 134447104 | bytes 3145728 | tf_op jit(solution)/shard_map/tf,cfg->ctg/dot_general | solution.py:91
  95.9 0.7 fusion.56
  96.5 0.7 fusion.59
  98.1 2.1 %multiply_reduce_fusion = (f32[]{:T(128)}, f32[256,8,128]{2,0,1:T(8,128)}) fusion(f32[256,8,128]{2,0,1:T(8,128)S(1)} %fusion.1, f32[8,512,128]{2,1,0:T(8,128)S(1)} %fusion.59, f32[8,512,128]{2,1,0:T(8,128)S(1)} %fusion.56, f32[128,512]{0,1:T(8,128)S(1)} %get-tuple-element.28, f32[128,512]{0,1:T(8,128)S(1)} %get-tuple-element.29, ...), kind=kOutput, calls=%fused_computation.108 | convolution fusion | flops 271056896 | bytes 7077892 | tf_op jit(solution)/shard_map/ckg,gt->ctk/dot_general | solution.py:98
  100.2 1.3 broadcast_in_dim.8
  101.5 3.9 %all-to-all-start.5 = ((f32[32,1,1]{2,1,0:T(1,128)}), f32[32,1,1]{2,1,0:T(1,128)S(1)}, u32[]{:S(2)}, u32[]{:S(2)}) async-start(f32[32,1,1]{2,1,0:T(1,128)} %broadcast_in_dim.8), calls=%async_computation.5 | async-start | bytes 32768 | tf_op jit(solution)/shard_map/all_to_all | solution.py:20
  105.4 2.4 %fusion.44 = f32[8,512,128]{2,1,0:T(8,128)S(1)} fusion(f32[8,512,128]{2,1,0:T(8,128)} %fusion.36, bf16[8,512,128]{2,1,0:T(8,128)(2,1)S(1)} %copy-done.5), kind=kOutput, calls=%fused_computation.64 | convolution fusion | flops 134971392 | bytes 5242880 | tf_op jit(solution)/shard_map/tf,cfg->ctg/dot_general | solution.py:89
  107.8 0.7 fusion.47
  109.0 1.6 fusion.68
  110.6 2.5 %mul.883 = f32[8,32,1024]{2,1,0:T(8,128)} reshape(f32[8,256,128]{2,1,0:T(8,128)} %fusion.68) | data formatting | bytes 2097152 | tf_op jit(solution)/shard_map/mul | solution.py:100
  113.1 2.4 %fusion.50 = f32[8,512,128]{2,1,0:T(8,128)S(1)} fusion(f32[8,512,128]{2,1,0:T(8,128)} %fusion.22, bf16[8,512,128]{2,1,0:T(8,128)(2,1)S(1)} %copy-done.4), kind=kOutput, calls=%fused_computation.66 | convolution fusion | flops 134971392 | bytes 5242880 | tf_op jit(solution)/shard_map/tf,cfg->ctg/dot_general | solution.py:89
  115.5 0.7 fusion.53
  117.3 1.2 mul.900
  119.0 3.4 %fusion.94 = (bf16[8,32,1024]{2,0,1:T(8,128)(2,1)}, bf16[8,32,1024]{2,0,1:T(8,128)(2,1)S(1)}) fusion(f32[8,32,1024]{2,1,0:T(8,128)} %mul.900, f32[8]{0:T(128)S(1)} %copy-done.25, bf16[32,8,1024]{2,1,0:T(8,128)(2,1)} %all-to-all-done.3, bf16[32,8,1024]{2,1,0:T(8,128)(2,1)S(1)} %copy-done.15, f32[8,32,1024]{2,1,0:T(8,128)S(1)} %copy-done.20), kind=kLoop, calls=%fused_computation.103 | loop fusion | flops 2097152 | bytes 4194336 | tf_op jit(solution)/shard_map/convert_element_type | solution.py:146
  122.4 18.9 %all_to_all.74 = bf16[8,32,1024]{2,0,1:T(8,128)(2,1)S(1)} all-to-all(bf16[8,32,1024]{2,0,1:T(8,128)(2,1)S(1)} %get-tuple-element.25), channel_id=1, replica_groups=mesh['ex'=8,'ctx'=32] {'ctx'}, dimensions={1} | all-to-all | bytes 1048576 | tf_op jit(solution)/shard_map/all_to_all | solution.py:161
  141.4 3.7 %all-to-all-start.4 = ((bf16[8,32,1024]{2,0,1:T(8,128)(2,1)}), bf16[8,32,1024]{2,0,1:T(8,128)(2,1)S(1)}, u32[]{:S(2)}, u32[]{:S(2)}) async-start(bf16[8,32,1024]{2,0,1:T(8,128)(2,1)} %get-tuple-element.24), calls=%async_computation.4 | async-start | bytes 1048576 | tf_op jit(solution)/shard_map/all_to_all | solution.py:162
  145.7 0.7 reduce_sum.28
  147.4 1.1 copy.190
  148.5 8.1 %all-to-all-done.4 = bf16[8,32,1024]{2,0,1:T(8,128)(2,1)S(1)} async-done(((bf16[8,32,1024]{2,0,1:T(8,128)(2,1)}), bf16[8,32,1024]{2,0,1:T(8,128)(2,1)S(1)}, u32[]{:S(2)}, u32[]{:S(2)}) %all-to-all-start.4) | async-done | bytes 524320 | tf_op jit(solution)/shard_map/all_to_all | solution.py:162
  156.6 6.9 %all-to-all-start.6 = ((bf16[8,8,4096]{2,1,0:T(8,128)(2,1)}), bf16[8,8,4096]{2,1,0:T(8,128)(2,1)S(1)}, u32[]{:S(2)}, u32[]{:S(2)}) async-start(bf16[8,8,4096]{2,1,0:T(8,128)(2,1)} %bitcast.285), calls=%async_computation.6 | async-start | bytes 1048576 | tf_op jit(solution)/shard_map/all_to_all | solution.py:38
  164.3 1.0 copy.159
  165.3 16.3 %all-to-all-done.6 = bf16[8,8,4096]{2,1,0:T(8,128)(2,1)S(1)} async-done(((bf16[8,8,4096]{2,1,0:T(8,128)(2,1)}), bf16[8,8,4096]{2,1,0:T(8,128)(2,1)S(1)}, u32[]{:S(2)}, u32[]{:S(2)}) %all-to-all-start.6) | async-done | bytes 524320 | tf_op jit(solution)/shard_map/all_to_all | solution.py:38
  181.6 0.7 convert_reduce_fusion
  (63 shorter events, 6.5 us)
Async XLA Ops:
  0.6 1.1 copy-start
  0.6 11.9 %copy-start.24 = (f32[8,4096]{1,0:T(8,128)S(1)}, f32[8,4096]{1,0:T(8,128)}, u32[]{:S(2)}) copy-start(f32[8,4096]{1,0:T(8,128)} %param.14) | copy-start | bytes 393220
  1.7 21.1 %copy-start.22 = (bf16[256,256]{1,0:T(8,128)(2,1)S(1)}, bf16[256,256]{1,0:T(8,128)(2,1)}, u32[]{:S(2)}) copy-start(bf16[256,256]{1,0:T(8,128)(2,1)} %param.12) | copy-start | bytes 393220
  4.0 20.2 %all-to-all-start.1 = ((bf16[32,8,1024]{2,1,0:T(8,128)(2,1)}), bf16[32,8,1024]{2,1,0:T(8,128)(2,1)S(1)}, u32[]{:S(2)}, u32[]{:S(2)}) async-start(bf16[32,8,1024]{2,1,0:T(8,128)(2,1)} %fusion.88), calls=%async_computation.1 | async-start | bytes 1048576 | tf_op jit(solution)/shard_map/all_to_all | solution.py:133
  24.1 7.5 %copy-start.14 = (bf16[32,8,1024]{2,1,0:T(8,128)(2,1)}, bf16[32,8,1024]{2,1,0:T(8,128)(2,1)S(1)}, u32[]{:S(2)}) copy-start(bf16[32,8,1024]{2,1,0:T(8,128)(2,1)S(1)} %all-to-all-done.1) | copy-start | bytes 1572868
  24.1 18.8 %all-to-all-start.3 = ((bf16[32,8,1024]{2,1,0:T(8,128)(2,1)}), bf16[32,8,1024]{2,1,0:T(8,128)(2,1)}, u32[]{:S(2)}, u32[]{:S(2)}) async-start(bf16[32,8,1024]{2,1,0:T(8,128)(2,1)} %fusion.89), calls=%async_computation.3 | async-start | bytes 1048576 | tf_op jit(solution)/shard_map/all_to_all | solution.py:132
  31.6 2.7 %copy-start.6 = (bf16[512,512]{0,1:T(8,128)(2,1)S(1)}, bf16[512,512]{0,1:T(8,128)(2,1)}, u32[]{:S(2)}) copy-start(bf16[512,512]{0,1:T(8,128)(2,1)} %fusion.119) | copy-start | bytes 1572868
  32.7 1.6 copy-start.16
  43.8 26.5 %all-to-all-start = ((bf16[8,8,4096]{2,1,0:T(8,128)(2,1)}), bf16[8,8,4096]{2,1,0:T(8,128)(2,1)}, u32[]{:S(2)}, u32[]{:S(2)}) async-start(bf16[8,8,4096]{2,1,0:T(8,128)(2,1)} %broadcast_in_dim.6), calls=%async_computation | async-start | bytes 1048576 | tf_op jit(solution)/shard_map/all_to_all | solution.py:20
  56.2 1.6 copy-start.17
  59.0 1.6 copy-start.2
  74.5 1.6 copy-start.18
  78.2 1.8 %copy-start.10 = (f32[8,512,128]{2,1,0:T(8,128)S(1)}, f32[8,512,128]{2,1,0:T(8,128)}, u32[]{:S(2)}) copy-start(f32[8,512,128]{2,1,0:T(8,128)} %fusion.128) | copy-start | bytes 6291460
  79.1 1.8 copy-start.3
  79.1 2.4 %copy-start.7 = (f32[8,512,128]{2,1,0:T(8,128)S(1)}, f32[8,512,128]{2,1,0:T(8,128)}, u32[]{:S(2)}) copy-start(f32[8,512,128]{2,1,0:T(8,128)} %convolution_add_fusion.1) | copy-start | bytes 6291460
  79.1 3.0 %copy-start.8 = (f32[8,512,128]{2,1,0:T(8,128)S(1)}, f32[8,512,128]{2,1,0:T(8,128)}, u32[]{:S(2)}) copy-start(f32[8,512,128]{2,1,0:T(8,128)} %convolution_add_fusion) | copy-start | bytes 6291460
  79.1 3.6 %copy-start.9 = (f32[8,512,128]{2,1,0:T(8,128)S(1)}, f32[8,512,128]{2,1,0:T(8,128)}, u32[]{:S(2)}) copy-start(f32[8,512,128]{2,1,0:T(8,128)} %convolution_subtract_fusion) | copy-start | bytes 6291460
  96.5 1.0 copy-start.13
  98.0 7.3 %copy-start.5 = (bf16[8,512,128]{2,1,0:T(8,128)(2,1)S(1)}, bf16[8,512,128]{2,1,0:T(8,128)(2,1)}, u32[]{:S(2)}) copy-start(bf16[8,512,128]{2,1,0:T(8,128)(2,1)} %get-tuple-element.23) | copy-start | bytes 3145732
  101.5 21.0 %all-to-all-start.5 = ((f32[32,1,1]{2,1,0:T(1,128)}), f32[32,1,1]{2,1,0:T(1,128)S(1)}, u32[]{:S(2)}, u32[]{:S(2)}) async-start(f32[32,1,1]{2,1,0:T(1,128)} %broadcast_in_dim.8), calls=%async_computation.5 | async-start | bytes 32768 | tf_op jit(solution)/shard_map/all_to_all | solution.py:20
  105.4 2.4 %copy-start.12 = (f32[8,512,128]{2,1,0:T(8,128)S(1)}, f32[8,512,128]{2,1,0:T(8,128)}, u32[]{:S(2)}) copy-start(f32[8,512,128]{2,1,0:T(8,128)} %fusion.34) | copy-start | bytes 6291460
  110.6 2.5 %copy-start.4 = (bf16[8,512,128]{2,1,0:T(8,128)(2,1)S(1)}, bf16[8,512,128]{2,1,0:T(8,128)(2,1)}, u32[]{:S(2)}) copy-start(bf16[8,512,128]{2,1,0:T(8,128)(2,1)} %get-tuple-element.21) | copy-start | bytes 3145732
  113.1 2.4 %copy-start.11 = (f32[8,512,128]{2,1,0:T(8,128)S(1)}, f32[8,512,128]{2,1,0:T(8,128)}, u32[]{:S(2)}) copy-start(f32[8,512,128]{2,1,0:T(8,128)} %fusion.20) | copy-start | bytes 6291460
  117.3 1.2 copy-start.15
  117.3 1.8 copy-start.20
  117.3 1.8 copy-start.25
  122.4 24.6 %copy-start.19 = (f32[256,8,128]{2,0,1:T(8,128)S(1)}, f32[256,8,128]{2,0,1:T(8,128)}, u32[]{:S(2)}) copy-start(f32[256,8,128]{2,0,1:T(8,128)} %get-tuple-element.27) | copy-start | bytes 3145732
  141.4 15.2 %all-to-all-start.4 = ((bf16[8,32,1024]{2,0,1:T(8,128)(2,1)}), bf16[8,32,1024]{2,0,1:T(8,128)(2,1)S(1)}, u32[]{:S(2)}, u32[]{:S(2)}) async-start(bf16[8,32,1024]{2,0,1:T(8,128)(2,1)} %get-tuple-element.24), calls=%async_computation.4 | async-start | bytes 1048576 | tf_op jit(solution)/shard_map/all_to_all | solution.py:162
  147.4 16.4 %copy-start.21 = (bf16[1,256,1024]{2,1,0:T(8,128)(2,1)S(1)}, bf16[1,256,1024]{2,1,0:T(8,128)(2,1)}, u32[]{:S(2)}) copy-start(bf16[1,256,1024]{2,1,0:T(8,128)(2,1)} %param.9) | copy-start | bytes 1572868
  147.4 16.4 %copy-start.23 = (bf16[256,256]{1,0:T(8,128)(2,1)S(1)}, bf16[256,256]{1,0:T(8,128)(2,1)}, u32[]{:S(2)}) copy-start(bf16[256,256]{1,0:T(8,128)(2,1)} %param.13) | copy-start | bytes 393220
  156.6 25.0 %all-to-all-start.6 = ((bf16[8,8,4096]{2,1,0:T(8,128)(2,1)}), bf16[8,8,4096]{2,1,0:T(8,128)(2,1)S(1)}, u32[]{:S(2)}, u32[]{:S(2)}) async-start(bf16[8,8,4096]{2,1,0:T(8,128)(2,1)} %bitcast.285), calls=%async_computation.6 | async-start | bytes 1048576 | tf_op jit(solution)/shard_map/all_to_all | solution.py:38
  163.5 18.8 %copy-start.1 = (bf16[1,256,1024]{2,1,0:T(8,128)(2,1)S(1)}, bf16[1,256,1024]{2,1,0:T(8,128)(2,1)}, u32[]{:S(2)}) copy-start(bf16[1,256,1024]{2,1,0:T(8,128)(2,1)} %param.8) | copy-start | bytes 1572868
where the time goes:
time: 183 us; the launch traced here: 182 us
  matrix products  52.6 us (29%)
  starting transfers between devices  38.5 us (21%)
  waiting for transfers between devices  31.5 us (17%)
  local copies, waits for them, and re-layouts  22.5 us (12%)
  blocking collectives  18.9 us (10%)
  other arithmetic  15.9 us (9%)
  between operations  2.43 us (1%)
    all_to_all x1, blocking collectives, on_device(): lax.all_to_all(value_grad_ch, 'ctx', split_axis=1, concat_axis=0, tiled=T...  18.9 us
    all_to_all x1, waiting for transfers between devices, sum_at_owner(): parts = lax.all_to_all(cut_along(x, dim, size), axis, 0, 0, tiled=True)  16.3 us
    all_to_all x2, starting transfers between devices, from_everyone(): return lax.all_to_all(copies, axis, split_axis=0, concat_axis=0, tiled=True)  12.1 us
    all_to_all x1, starting transfers between devices, on_device(): lax.all_to_all(signal_tok, 'ctx', split_axis=0, concat_axis=1, tiled=True)  8.58 us
    all_to_all x1, waiting for transfers between devices, on_device(): lax.all_to_all(conv_state, 'ctx', split_axis=1, concat_axis=0, tiled=True)  8.05 us
    all_to_all x1, starting transfers between devices, on_device(): lax.all_to_all(value_tok, 'ctx', split_axis=0, concat_axis=1, tiled=True)  7.19 us
    all_to_all x1, starting transfers between devices, sum_at_owner(): parts = lax.all_to_all(cut_along(x, dim, size), axis, 0, 0, tiled=True)  6.92 us
    dot_general x3, matrix products, second_section(): out_imag = out_imag - jnp.einsum('fk,ckg->cfg', sin_short, twist_real)  6.9 us
  transfers between devices with their start and end apart: 6, of which 4 were waited for; matrix products, arithmetic and copies ran while one was open for 29% of the time, Pallas kernels for 0%

commit v1 on v0

--- a/solution.py
+++ b/solution.py
@@ -7,6 +7,13 @@
 RADIX = 128
 unknown_base = 4
 norm_eps = 1e-06
+
+
+def trade_parts(block, axis, split, join):
+    n_dev = lax.axis_size(axis)
+    blocks = jnp.stack(jnp.split(block, n_dev, axis=split), axis=0)
+    blocks = lax.all_to_all(blocks, axis, split_axis=0, concat_axis=0)
+    return jnp.concatenate(blocks, axis=join)
 
 
 def joined_along(parts, dim):
@@ -158,7 +165,7 @@
         half_blocks,
     )
     value_grad_tok, state_tok = (
-        lax.all_to_all(value_grad_ch, "ctx", split_axis=1, concat_axis=0, tiled=True),
+        trade_parts(value_grad_ch, "ctx", 1, 0),
         lax.all_to_all(conv_state, "ctx", split_axis=1, concat_axis=0, tiled=True),
     )
     gate_grad_tok = (state_tok.astype(jnp.float32) * cot_tok).astype(jnp.bfloat16)

time: 183 us -> 200 us (1.093)
  blocking collectives: 18.9 us -> 0 us
  local copies, waits for them, and re-layouts: 22.5 us -> 40.7 us
  waiting for transfers between devices: 31.5 us -> 41.3 us
  starting transfers between devices: 38.5 us -> 45.9 us
    all_to_all x1 -> x0, blocking collectives: 18.9 us -> none  [on_device(): lax.all_to_all(value_grad_ch, 'ctx', split_axis=1, concat_axis=0, tiled=T...]
    unnamed x53 -> x84, local copies, waits for them, and re-layouts: 5.75 us -> 24.4 us
    all_to_all x0 -> x1, waiting for transfers between devices: none -> 8.11 us  [trade_parts(): blocks = lax.all_to_all(blocks, axis, split_axis=0, concat_axis=0)]
    all_to_all x1, starting transfers between devices: 3.68 us -> 7.39 us  [on_device(): lax.all_to_all(conv_state, 'ctx', split_axis=1, concat_axis=0, tiled=True)]
    all_to_all x0 -> x1, starting transfers between devices: none -> 3.68 us  [trade_parts(): blocks = lax.all_to_all(blocks, axis, split_axis=0, concat_axis=0)]
  transfers between devices with their start and end apart: 6 -> 7, of which waited for: 4 -> 5; matrix products, arithmetic and copies ran while one was open for 29% -> 36% of each run, Pallas kernels for 0% -> 0%
where the time goes in v1:
time: 200 us; the launch traced here: 199 us
  matrix products  52.7 us (26%)
  starting transfers between devices  45.9 us (23%)
  waiting for transfers between devices  41.3 us (21%)
  local copies, waits for them, and re-layouts  40.7 us (20%)
  other arithmetic  15.6 us (8%)
  between operations  2.43 us (1%)
    unnamed x84, local copies, waits for them, and re-layouts  24.4 us
    all_to_all x1, waiting for transfers between devices, sum_at_owner(): parts = lax.all_to_all(cut_along(x, dim, size), axis, 0, 0, tiled=True)  16.3 us
    all_to_all x2, starting transfers between devices, from_everyone(): return lax.all_to_all(copies, axis, split_axis=0, concat_axis=0, tiled=True)  12.1 us
    all_to_all x1, waiting for transfers between devices, on_device(): lax.all_to_all(conv_state, 'ctx', split_axis=1, concat_axis=0, tiled=True)  9.77 us
    all_to_all x1, starting transfers between devices, on_device(): lax.all_to_all(signal_tok, 'ctx', split_axis=0, concat_axis=1, tiled=True)  8.58 us
    all_to_all x1, waiting for transfers between devices, trade_parts(): blocks = lax.all_to_all(blocks, axis, split_axis=0, concat_axis=0)  8.11 us
    all_to_all x1, starting transfers between devices, on_device(): lax.all_to_all(conv_state, 'ctx', split_axis=1, concat_axis=0, tiled=True)  7.39 us
    all_to_all x1, starting transfers between devices, on_device(): lax.all_to_all(value_tok, 'ctx', split_axis=0, concat_axis=1, tiled=True)  7.21 us
  transfers between devices with their start and end apart: 7, of which 5 were waited for; matrix products, arithmetic and copies ran while one was open for 36% of the time, Pallas kernels for 0%

profile of v1, /device:TPU:1, one launch (start us, length us, event | category | flops | bytes accessed | tf_op | source)
XLA Modules:
  0.0 198.5 jit_solution(15319207876102332047)
XLA Ops:
  0.7 0.8 compare_convert_fusion
  1.7 2.2 %fusion.88 = bf16[32,8,1024]{2,1,0:T(8,128)(2,1)} fusion(bf16[256,256]{1,0:T(8,128)(2,1)} %param.13, bf16[1,256,1024]{2,1,0:T(8,128)(2,1)} %param.9, bf16[1,256,1024]{2,1,0:T(8,128)(2,1)S(1)} %copy-done, f32[1024]{0:T(1024)S(1)} %bitcast.421), kind=kOutput, calls=%fused_computation.94 | convolution fusion | flops 135790592 | bytes 1708032 | tf_op jit(solution)/shard_map/dot_general | solution.py:113
  3.9 8.6 %all-to-all-start.1 = ((bf16[32,8,1024]{2,1,0:T(8,128)(2,1)}), bf16[32,8,1024]{2,1,0:T(8,128)(2,1)S(1)}, u32[]{:S(2)}, u32[]{:S(2)}) async-start(bf16[32,8,1024]{2,1,0:T(8,128)(2,1)} %fusion.88), calls=%async_computation.1 | async-start | bytes 1048576 | tf_op jit(solution)/shard_map/all_to_all | solution.py:140
  12.6 1.0 fusion.143
  13.6 4.6 %fusion.120 = bf16[512,512]{0,1:T(8,128)(2,1)} fusion(), kind=kLoop, calls=%fused_computation.138 | loop fusion | flops 3932160 | bytes 524288 | tf_op jit(solution)/shard_map/cos | solution.py:54
  18.2 4.6 %fusion.119 = bf16[512,512]{0,1:T(8,128)(2,1)} fusion(), kind=kLoop, calls=%fused_computation.137 | loop fusion | flops 3932160 | bytes 524288 | tf_op jit(solution)/shard_map/sin | solution.py:54
  22.8 1.1 fusion.89
  24.1 7.2 %all-to-all-start.3 = ((bf16[32,8,1024]{2,1,0:T(8,128)(2,1)}), bf16[32,8,1024]{2,1,0:T(8,128)(2,1)}, u32[]{:S(2)}, u32[]{:S(2)}) async-start(bf16[32,8,1024]{2,1,0:T(8,128)(2,1)} %fusion.89), calls=%async_computation.3 | async-start | bytes 1048576 | tf_op jit(solution)/shard_map/all_to_all | solution.py:139
  31.7 1.0 reshape.93
  32.7 1.6 fusion.122
  34.3 1.8 fusion.125
  36.1 6.9 %all-to-all-done.3 = bf16[32,8,1024]{2,1,0:T(8,128)(2,1)} async-done(((bf16[32,8,1024]{2,1,0:T(8,128)(2,1)}), bf16[32,8,1024]{2,1,0:T(8,128)(2,1)}, u32[]{:S(2)}, u32[]{:S(2)}) %all-to-all-start.3) | async-done | bytes 524320 | tf_op jit(solution)/shard_map/all_to_all | solution.py:139
  43.0 0.8 broadcast_in_dim.6
  43.8 8.2 %all-to-all-start = ((bf16[8,8,4096]{2,1,0:T(8,128)(2,1)}), bf16[8,8,4096]{2,1,0:T(8,128)(2,1)}, u32[]{:S(2)}, u32[]{:S(2)}) async-start(bf16[8,8,4096]{2,1,0:T(8,128)(2,1)} %broadcast_in_dim.6), calls=%async_computation | async-start | bytes 1048576 | tf_op jit(solution)/shard_map/all_to_all | solution.py:27
  52.0 2.1 %copy.115 = bf16[8,32,1024]{2,1,0:T(8,128)(2,1)} copy(bf16[8,32,1024]{2,0,1:T(8,128)(2,1)} %bitcast.56) | data formatting | bytes 1048576 | tf_op jit(solution)/shard_map/all_to_all | solution.py:139
  54.1 2.1 %reshape.95 = bf16[8,256,128]{2,1,0:T(8,128)(2,1)} reshape(bf16[8,32,1024]{2,1,0:T(8,128)(2,1)} %copy.115) | data formatting | bytes 1048576 | tf_op jit(solution)/shard_map/reshape | solution.py:70
  56.2 1.6 fusion.121
  58.3 0.8 fusion.129
  59.1 0.8 fusion.130
  59.9 0.8 copy-done.2
  60.6 0.8 fusion.127
  61.4 2.2 %convolution_add_fusion.1 = f32[8,512,128]{2,1,0:T(8,128)} fusion(f32[8,512,128]{2,1,0:T(8,128)S(1)} %fusion.127, f32[8,128,512]{1,2,0:T(8,128)S(1)} %fusion.122, f32[8,128,512]{1,2,0:T(8,128)S(1)} %copy-done.2, f32[128,512]{0,1:T(8,128)S(1)} %get-tuple-element.24, f32[128,512]{0,1:T(8,128)S(1)} %get-tuple-element.25), kind=kOutput, calls=%fused_computation.74 | convolution fusion | flops 137068544 | bytes 8912896 | tf_op jit(solution)/shard_map/fk,ckg->cfg/dot_general | solution.py:83
  63.7 2.1 %fusion.128 = f32[8,512,128]{2,1,0:T(8,128)} fusion(f32[8,128,512]{1,2,0:T(8,128)S(1)} %fusion.122, f32[8,128,512]{1,2,0:T(8,128)S(1)} %copy-done.2, f32[128,512]{0,1:T(8,128)S(1)} %get-tuple-element.24, f32[128,512]{0,1:T(8,128)S(1)} %get-tuple-element.25), kind=kOutput, calls=%fused_computation.149 | convolution fusion | flops 136544256 | bytes 6815744 | tf_op jit(solution)/shard_map/fk,ckg->cfg/dot_general | solution.py:84
  65.8 2.3 %convolution_add_fusion = f32[8,512,128]{2,1,0:T(8,128)} fusion(f32[8,512,128]{2,1,0:T(8,128)S(1)} %fusion.129, f32[8,128,512]{1,2,0:T(8,128)S(1)} %fusion.121, f32[8,128,512]{1,2,0:T(8,128)S(1)} %fusion.124, f32[128,512]{0,1:T(8,128)S(1)} %get-tuple-element.24, f32[128,512]{0,1:T(8,128)S(1)} %get-tuple-element.25), kind=kOutput, calls=%fused_computation.71 | convolution fusion | flops 137068544 | bytes 8912896 | tf_op jit(solution)/shard_map/fk,ckg->cfg/dot_general | solution.py:83
  68.1 2.2 %convolution_subtract_fusion = f32[8,512,128]{2,1,0:T(8,128)} fusion(f32[8,512,128]{2,1,0:T(8,128)S(1)} %fusion.130, f32[8,128,512]{1,2,0:T(8,128)S(1)} %fusion.121, f32[8,128,512]{1,2,0:T(8,128)S(1)} %fusion.124, f32[128,512]{0,1:T(8,128)S(1)} %get-tuple-element.24, f32[128,512]{0,1:T(8,128)S(1)} %get-tuple-element.25), kind=kOutput, calls=%fused_computation.70 | convolution fusion | flops 137068544 | bytes 8912896 | tf_op jit(solution)/shard_map/fk,ckg->cfg/dot_general | solution.py:85
  70.3 2.1 %copy.104 = bf16[8,8,4096]{2,1,0:T(8,128)(2,1)} copy(bf16[8,8,4096]{2,0,1:T(8,128)(2,1)} %bitcast.2) | data formatting | bytes 1048576 | tf_op jit(solution)/shard_map/transpose | solution.py:22
  72.4 2.1 %reshape.92 = bf16[8,256,128]{2,1,0:T(8,128)(2,1)} reshape(bf16[8,8,4096]{2,1,0:T(8,128)(2,1)} %copy.104) | data formatting | bytes 1048576 | tf_op jit(solution)/shard_map/reshape | solution.py:70
  74.5 1.6 fusion.123
  76.6 0.8 fusion.135
  77.4 0.8 fusion.131
  78.2 0.9 convolution_add_fusion.2
  79.1 0.9 convolution_subtract_fusion.2
  80.0 0.8 copy-done.3
  80.9 0.6 copy-done.7
  82.7 3.8 %multiply_add_fusion = (bf16[8,512,128]{2,1,0:T(8,128)(2,1)S(1)}, bf16[8,512,128]{2,1,0:T(8,128)(2,1)S(1)}, bf16[8,512,128]{2,1,0:T(8,128)(2,1)S(1)}, bf16[8,512...) fusion(f32[8,512,128]{2,1,0:T(8,128)S(1)} %copy-done.9, ...), kind=kOutput, calls=%fused_computation.55 | convolution fusion | flops 149651456 | bytes 23592960 | tf_op jit(solution)/shard_map/fk,ckg->cfg/dot_general | solution.py:85
  86.5 0.7 fusion.8
  87.2 0.7 fusion.6
  87.8 2.1 %fusion.22 = f32[8,512,128]{2,1,0:T(8,128)} fusion(bf16[8,512,128]{2,1,0:T(8,128)(2,1)S(1)} %get-tuple-element.18), kind=kOutput, calls=%fused_computation.26 | convolution fusion | flops 134447104 | bytes 3145728 | tf_op jit(solution)/shard_map/tf,cfg->ctg/dot_general | solution.py:97
  89.9 2.0 %fusion.20 = f32[8,512,128]{2,1,0:T(8,128)} fusion(bf16[8,512,128]{2,1,0:T(8,128)(2,1)S(1)} %get-tuple-element.18), kind=kOutput, calls=%fused_computation.24 | convolution fusion | flops 134447104 | bytes 3145728 | tf_op jit(solution)/shard_map/tf,cfg->ctg/dot_general | solution.py:98
  92.0 2.0 %fusion.36 = f32[8,512,128]{2,1,0:T(8,128)} fusion(bf16[8,512,128]{2,1,0:T(8,128)(2,1)S(1)} %get-tuple-element.20), kind=kOutput, calls=%fused_computation.42 | convolution fusion | flops 134447104 | bytes 3145728 | tf_op jit(solution)/shard_map/tf,cfg->ctg/dot_general | solution.py:97
  94.0 2.0 %fusion.34 = f32[8,512,128]{2,1,0:T(8,128)} fusion(bf16[8,512,128]{2,1,0:T(8,128)(2,1)S(1)} %get-tuple-element.20), kind=kOutput, calls=%fused_computation.40 | convolution fusion | flops 134447104 | bytes 3145728 | tf_op jit(solution)/shard_map/tf,cfg->ctg/dot_general | solution.py:98
  96.0 0.7 fusion.56
  96.6 0.7 fusion.59
  98.2 2.1 %multiply_reduce_fusion = (f32[]{:T(128)}, f32[256,8,128]{2,0,1:T(8,128)}) fusion(f32[256,8,128]{2,0,1:T(8,128)S(1)} %fusion.1, f32[8,512,128]{2,1,0:T(8,128)S(1)} %fusion.59, f32[8,512,128]{2,1,0:T(8,128)S(1)} %fusion.56, f32[128,512]{0,1:T(8,128)S(1)} %get-tuple-element.24, f32[128,512]{0,1:T(8,128)S(1)} %get-tuple-element.25, ...), kind=kOutput, calls=%fused_computation.109 | convolution fusion | flops 271056896 | bytes 7077892 | tf_op jit(solution)/shard_map/ckg,gt->ctk/dot_general | solution.py:105
  100.3 1.3 broadcast_in_dim.8
  101.6 3.9 %all-to-all-start.5 = ((f32[32,1,1]{2,1,0:T(1,128)}), f32[32,1,1]{2,1,0:T(1,128)S(1)}, u32[]{:S(2)}, u32[]{:S(2)}) async-start(f32[32,1,1]{2,1,0:T(1,128)} %broadcast_in_dim.8), calls=%async_computation.5 | async-start | bytes 32768 | tf_op jit(solution)/shard_map/all_to_all | solution.py:27
  105.5 2.4 %fusion.50 = f32[8,512,128]{2,1,0:T(8,128)S(1)} fusion(f32[8,512,128]{2,1,0:T(8,128)} %fusion.22, bf16[8,512,128]{2,1,0:T(8,128)(2,1)S(1)} %copy-done.5), kind=kOutput, calls=%fused_computation.66 | convolution fusion | flops 134971392 | bytes 5242880 | tf_op jit(solution)/shard_map/tf,cfg->ctg/dot_general | solution.py:96
  107.9 0.7 fusion.53
  109.1 1.6 fusion.77
  110.7 2.5 %mul.900 = f32[8,32,1024]{2,1,0:T(8,128)} reshape(f32[8,256,128]{2,1,0:T(8,128)} %fusion.77) | data formatting | bytes 2097152 | tf_op jit(solution)/shard_map/mul | solution.py:107
  113.2 2.4 %fusion.44 = f32[8,512,128]{2,1,0:T(8,128)S(1)} fusion(f32[8,512,128]{2,1,0:T(8,128)} %fusion.36, bf16[8,512,128]{2,1,0:T(8,128)(2,1)S(1)} %copy-done.4), kind=kOutput, calls=%fused_computation.64 | convolution fusion | flops 134971392 | bytes 5242880 | tf_op jit(solution)/shard_map/tf,cfg->ctg/dot_general | solution.py:96
  115.6 0.7 fusion.47
  135.5 2.5 %fusion.95 = bf16[8,32,1024]{2,0,1:T(8,128)(2,1)} fusion(f32[8,32,1024]{2,1,0:T(8,128)S(1)} %copy-done.20, f32[8]{0:T(128)S(1)} %copy-done.25, bf16[32,8,1024]{2,1,0:T(8,128)(2,1)} %all-to-all-done.3), kind=kLoop, calls=%fused_computation.106 | loop fusion | flops 1048576 | bytes 2097184 | tf_op jit(solution)/shard_map/convert_element_type | solution.py:153
  138.6 7.4 %all-to-all-start.4 = ((bf16[8,32,1024]{2,0,1:T(8,128)(2,1)}), bf16[8,32,1024]{2,0,1:T(8,128)(2,1)S(1)}, u32[]{:S(2)}, u32[]{:S(2)}) async-start(bf16[8,32,1024]{2,0,1:T(8,128)(2,1)} %fusion.95), calls=%async_computation.4 | async-start | bytes 1048576 | tf_op jit(solution)/shard_map/all_to_all | solution.py:169
  146.0 0.6 constant_dynamic-update-slice_fusion.2
  147.8 9.8 %all-to-all-done.4 = bf16[8,32,1024]{2,0,1:T(8,128)(2,1)S(1)} async-done(((bf16[8,32,1024]{2,0,1:T(8,128)(2,1)}), bf16[8,32,1024]{2,0,1:T(8,128)(2,1)S(1)}, u32[]{:S(2)}, u32[]{:S(2)}) %all-to-all-start.4) | async-done | bytes 524320 | tf_op jit(solution)/shard_map/all_to_all | solution.py:169
  157.6 3.7 %all-to-all-start.2 = ((bf16[32,8,1024]{2,1,0:T(8,128)(2,1)}), bf16[32,8,1024]{2,1,0:T(8,128)(2,1)S(1)}, u32[]{:S(2)}, u32[]{:S(2)}) async-start(bf16[32,8,1024]{2,1,0:T(8,128)(2,1)} %constant_dynamic-update-slice_fusion), calls=%async_computation.2 | async-start | bytes 1048576 | tf_op jit(solution)/shard_map/all_to_all | solution.py:15
  161.9 0.7 reduce_sum.28
  163.6 1.1 copy.160
  164.7 8.1 %all-to-all-done.2 = bf16[32,8,1024]{2,1,0:T(8,128)(2,1)S(1)} async-done(((bf16[32,8,1024]{2,1,0:T(8,128)(2,1)}), bf16[32,8,1024]{2,1,0:T(8,128)(2,1)S(1)}, u32[]{:S(2)}, u32[]{:S(2)}) %all-to-all-start.2) | async-done | bytes 524320 | tf_op jit(solution)/shard_map/all_to_all | solution.py:15
  172.8 6.9 %all-to-all-start.6 = ((bf16[8,8,4096]{2,1,0:T(8,128)(2,1)}), bf16[8,8,4096]{2,1,0:T(8,128)(2,1)S(1)}, u32[]{:S(2)}, u32[]{:S(2)}) async-start(bf16[8,8,4096]{2,1,0:T(8,128)(2,1)} %bitcast.418), calls=%async_computation.6 | async-start | bytes 1048576 | tf_op jit(solution)/shard_map/all_to_all | solution.py:45
  180.5 1.0 copy.130
  181.5 16.3 %all-to-all-done.6 = bf16[8,8,4096]{2,1,0:T(8,128)(2,1)S(1)} async-done(((bf16[8,8,4096]{2,1,0:T(8,128)(2,1)}), bf16[8,8,4096]{2,1,0:T(8,128)(2,1)S(1)}, u32[]{:S(2)}, u32[]{:S(2)}) %all-to-all-start.6) | async-done | bytes 524320 | tf_op jit(solution)/shard_map/all_to_all | solution.py:45
  197.8 0.7 convert_reduce_fusion
  (96 shorter events, 26.3 us)
Async XLA Ops:
  0.6 1.1 copy-start
  0.6 11.9 %copy-start.24 = (f32[8,4096]{1,0:T(8,128)S(1)}, f32[8,4096]{1,0:T(8,128)}, u32[]{:S(2)}) copy-start(f32[8,4096]{1,0:T(8,128)} %param.14) | copy-start | bytes 393220
  1.7 21.1 %copy-start.22 = (bf16[256,256]{1,0:T(8,128)(2,1)S(1)}, bf16[256,256]{1,0:T(8,128)(2,1)}, u32[]{:S(2)}) copy-start(bf16[256,256]{1,0:T(8,128)(2,1)} %param.12) | copy-start | bytes 393220
  3.9 20.2 %all-to-all-start.1 = ((bf16[32,8,1024]{2,1,0:T(8,128)(2,1)}), bf16[32,8,1024]{2,1,0:T(8,128)(2,1)S(1)}, u32[]{:S(2)}, u32[]{:S(2)}) async-start(bf16[32,8,1024]{2,1,0:T(8,128)(2,1)} %fusion.88), calls=%async_computation.1 | async-start | bytes 1048576 | tf_op jit(solution)/shard_map/all_to_all | solution.py:140
  24.1 7.5 %copy-start.14 = (bf16[32,8,1024]{2,1,0:T(8,128)(2,1)}, bf16[32,8,1024]{2,1,0:T(8,128)(2,1)S(1)}, u32[]{:S(2)}) copy-start(bf16[32,8,1024]{2,1,0:T(8,128)(2,1)S(1)} %all-to-all-done.1) | copy-start | bytes 1572868
  24.1 18.9 %all-to-all-start.3 = ((bf16[32,8,1024]{2,1,0:T(8,128)(2,1)}), bf16[32,8,1024]{2,1,0:T(8,128)(2,1)}, u32[]{:S(2)}, u32[]{:S(2)}) async-start(bf16[32,8,1024]{2,1,0:T(8,128)(2,1)} %fusion.89), calls=%async_computation.3 | async-start | bytes 1048576 | tf_op jit(solution)/shard_map/all_to_all | solution.py:139
  31.7 2.6 %copy-start.6 = (bf16[512,512]{0,1:T(8,128)(2,1)S(1)}, bf16[512,512]{0,1:T(8,128)(2,1)}, u32[]{:S(2)}) copy-start(bf16[512,512]{0,1:T(8,128)(2,1)} %fusion.119) | copy-start | bytes 1572868
  32.7 1.6 copy-start.16
  43.8 26.5 %all-to-all-start = ((bf16[8,8,4096]{2,1,0:T(8,128)(2,1)}), bf16[8,8,4096]{2,1,0:T(8,128)(2,1)}, u32[]{:S(2)}, u32[]{:S(2)}) async-start(bf16[8,8,4096]{2,1,0:T(8,128)(2,1)} %broadcast_in_dim.6), calls=%async_computation | async-start | bytes 1048576 | tf_op jit(solution)/shard_map/all_to_all | solution.py:27
  56.2 1.6 copy-start.17
  59.1 1.6 copy-start.2
  74.5 1.6 copy-start.18
  78.2 1.8 copy-start.10
  79.1 1.8 copy-start.3
  79.1 2.4 %copy-start.7 = (f32[8,512,128]{2,1,0:T(8,128)S(1)}, f32[8,512,128]{2,1,0:T(8,128)}, u32[]{:S(2)}) copy-start(f32[8,512,128]{2,1,0:T(8,128)} %convolution_add_fusion.1) | copy-start | bytes 6291460
  79.1 3.0 %copy-start.8 = (f32[8,512,128]{2,1,0:T(8,128)S(1)}, f32[8,512,128]{2,1,0:T(8,128)}, u32[]{:S(2)}) copy-start(f32[8,512,128]{2,1,0:T(8,128)} %convolution_add_fusion) | copy-start | bytes 6291460
  79.1 3.6 %copy-start.9 = (f32[8,512,128]{2,1,0:T(8,128)S(1)}, f32[8,512,128]{2,1,0:T(8,128)}, u32[]{:S(2)}) copy-start(f32[8,512,128]{2,1,0:T(8,128)} %convolution_subtract_fusion) | copy-start | bytes 6291460
  96.6 1.0 copy-start.13
  98.2 7.3 %copy-start.5 = (bf16[8,512,128]{2,1,0:T(8,128)(2,1)S(1)}, bf16[8,512,128]{2,1,0:T(8,128)(2,1)}, u32[]{:S(2)}) copy-start(bf16[8,512,128]{2,1,0:T(8,128)(2,1)} %get-tuple-element.19) | copy-start | bytes 3145732
  101.6 37.1 %all-to-all-start.5 = ((f32[32,1,1]{2,1,0:T(1,128)}), f32[32,1,1]{2,1,0:T(1,128)S(1)}, u32[]{:S(2)}, u32[]{:S(2)}) async-start(f32[32,1,1]{2,1,0:T(1,128)} %broadcast_in_dim.8), calls=%async_computation.5 | async-start | bytes 32768 | tf_op jit(solution)/shard_map/all_to_all | solution.py:27
  105.5 2.4 %copy-start.12 = (f32[8,512,128]{2,1,0:T(8,128)S(1)}, f32[8,512,128]{2,1,0:T(8,128)}, u32[]{:S(2)}) copy-start(f32[8,512,128]{2,1,0:T(8,128)} %fusion.20) | copy-start | bytes 6291460
  110.7 2.5 %copy-start.4 = (bf16[8,512,128]{2,1,0:T(8,128)(2,1)S(1)}, bf16[8,512,128]{2,1,0:T(8,128)(2,1)}, u32[]{:S(2)}) copy-start(bf16[8,512,128]{2,1,0:T(8,128)(2,1)} %get-tuple-element.21) | copy-start | bytes 3145732
  113.2 2.4 %copy-start.11 = (f32[8,512,128]{2,1,0:T(8,128)S(1)}, f32[8,512,128]{2,1,0:T(8,128)}, u32[]{:S(2)}) copy-start(f32[8,512,128]{2,1,0:T(8,128)} %fusion.34) | copy-start | bytes 6291460
  116.8 1.0 copy-start.15
  116.8 1.0 copy-start.25
  117.4 18.1 %copy-start.20 = (f32[8,32,1024]{2,1,0:T(8,128)S(1)}, f32[8,32,1024]{2,1,0:T(8,128)}, u32[]{:S(2)}) copy-start(f32[8,32,1024]{2,1,0:T(8,128)} %mul.900) | copy-start | bytes 3145732
  135.5 27.8 %copy-start.19 = (f32[256,8,128]{2,0,1:T(8,128)S(1)}, f32[256,8,128]{2,0,1:T(8,128)}, u32[]{:S(2)}) copy-start(f32[256,8,128]{2,0,1:T(8,128)} %get-tuple-element.23) | copy-start | bytes 3145732
  138.6 19.0 %all-to-all-start.4 = ((bf16[8,32,1024]{2,0,1:T(8,128)(2,1)}), bf16[8,32,1024]{2,0,1:T(8,128)(2,1)S(1)}, u32[]{:S(2)}, u32[]{:S(2)}) async-start(bf16[8,32,1024]{2,0,1:T(8,128)(2,1)} %fusion.95), calls=%async_computation.4 | async-start | bytes 1048576 | tf_op jit(solution)/shard_map/all_to_all | solution.py:169
  157.6 15.2 %all-to-all-start.2 = ((bf16[32,8,1024]{2,1,0:T(8,128)(2,1)}), bf16[32,8,1024]{2,1,0:T(8,128)(2,1)S(1)}, u32[]{:S(2)}, u32[]{:S(2)}) async-start(bf16[32,8,1024]{2,1,0:T(8,128)(2,1)} %constant_dynamic-update-slice_fusion), calls=%async_computation.2 | async-start | bytes 1048576 | tf_op jit(solution)/shard_map/all_to_all | solution.py:15
  163.6 16.5 %copy-start.21 = (bf16[1,256,1024]{2,1,0:T(8,128)(2,1)S(1)}, bf16[1,256,1024]{2,1,0:T(8,128)(2,1)}, u32[]{:S(2)}) copy-start(bf16[1,256,1024]{2,1,0:T(8,128)(2,1)} %param.9) | copy-start | bytes 1572868
  163.6 16.5 %copy-start.23 = (bf16[256,256]{1,0:T(8,128)(2,1)S(1)}, bf16[256,256]{1,0:T(8,128)(2,1)}, u32[]{:S(2)}) copy-start(bf16[256,256]{1,0:T(8,128)(2,1)} %param.13) | copy-start | bytes 393220
  172.8 25.0 %all-to-all-start.6 = ((bf16[8,8,4096]{2,1,0:T(8,128)(2,1)}), bf16[8,8,4096]{2,1,0:T(8,128)(2,1)S(1)}, u32[]{:S(2)}, u32[]{:S(2)}) async-start(bf16[8,8,4096]{2,1,0:T(8,128)(2,1)} %bitcast.418), calls=%async_computation.6 | async-start | bytes 1048576 | tf_op jit(solution)/shard_map/all_to_all | solution.py:45
  179.8 18.8 %copy-start.1 = (bf16[1,256,1024]{2,1,0:T(8,128)(2,1)S(1)}, bf16[1,256,1024]{2,1,0:T(8,128)(2,1)}, u32[]{:S(2)}) copy-start(bf16[1,256,1024]{2,1,0:T(8,128)(2,1)} %param.8) | copy-start | bytes 1572868
